TPU v7x, 32 devices: a whole 2x2x4 slice. The times are simulated.
32 devices in a mesh: dp: 8 (over y, x, core), mp: 4 (over z).
Axes of the slice: x: 2, y: 2, z: 4, core: 2. Of those that a mesh axis runs over, the one named last changes fastest.
Arguments:
- tokens: bfloat16 [1024, 8192], P(('dp', 'mp')), parts along dimension 0, may hold values from -6 to 6
- norm_gain: float32 [8192], replicated, may hold values from 0.5 to 1.5
- qkv_weight: bfloat16 [8192, 10240], P(None, 'mp'), may hold values from -0.0625 to 0.0625
- qkv_bias: float32 [10240], P('mp'), may hold values from -3 to 3
- qkv_grad: bfloat16 [1024, 10240], P('dp', 'mp'), parts along dimension 0, may hold values from -6 to 6
Outputs:
- qkv: bfloat16 [1024, 10240], P('dp', 'mp'), parts along dimension 0
- tokens_grad: float32 [1024, 8192], P(('dp', 'mp')), parts along dimension 0
- gain_grad: float32 [65536], P('dp'), parts along dimension 0
- bias_grad: float32 [81920], P(('dp', 'mp')), parts along dimension 0
There are 8 independent parts, one for each index of `dp`. A program takes and returns all parts, laid end to end along the dimension named above; an argument that names none is the same for every part. Nothing has to cross between parts.
All inputs are finite; a program needn't handle non-finite values.
Results may differ from a plain program's by a relative error of at most 0.0046.
Values may be sent and summed in bfloat16 or wider, within the bound.
A program may use at most 128 MiB of HBM per device.

v0:
```python
import jax
import jax.numpy as jnp
from jax import lax
from jax.sharding import PartitionSpec as P

HEAD_DIM = 128
SEQ_LEN = 32768
GROUP = 10
TOK_DEV = 32


def rotate_heads(joined, first_col, position, sign):
    rows, cols = joined.shape
    heads = cols // HEAD_DIM
    half = HEAD_DIM // 2
    parts = joined.reshape(rows, heads, 2, half)
    inverse = jnp.exp(
        -jnp.log(jnp.float32(1000000.0)) * (2.0 * jnp.arange(half).astype(jnp.float32) / HEAD_DIM)
    )
    angle = position.astype(jnp.float32)[:, None] * inverse[None, :]
    cosine = jnp.cos(angle)[:, None, :]
    sine = sign * jnp.sin(angle)[:, None, :]
    first = parts[:, :, 0, :]
    second = parts[:, :, 1, :]
    turned = jnp.stack([first * cosine - second * sine, second * cosine + first * sine], axis=2)
    head_index = first_col // HEAD_DIM + jnp.arange(heads)
    rotated = head_index % GROUP != GROUP - 1
    result = jnp.where(rotated[None, :, None, None], turned, parts)
    return result.reshape(rows, cols)


def positions(rows, stride):
    row_index = jnp.arange(rows)
    return row_index // TOK_DEV * stride + row_index % TOK_DEV


def normalize(tokens, norm_gain):
    values = tokens.astype(jnp.float32)
    scale = lax.rsqrt(jnp.mean(values * values, axis=1, keepdims=True) + 1e-06)
    return (values * scale * norm_gain[None, :]).astype(jnp.bfloat16)


def shards(tokens, norm_gain, qkv_weight, qkv_bias, qkv_grad):
    width = qkv_weight.shape[1]
    first_col = lax.axis_index("mp") * width
    stride = SEQ_LEN // lax.axis_size("mp")
    place = positions(qkv_grad.shape[0], stride)
    joined_grad = rotate_heads(qkv_grad.astype(jnp.float32), first_col, place, -1.0)
    bias_grad = jnp.sum(joined_grad, axis=0)
    joined_low = joined_grad.astype(jnp.bfloat16)
    normed_grad = lax.psum_scatter(
        lax.dot_general(
            joined_low, qkv_weight, (((1,), (1,)), ((), ())), preferred_element_type=jnp.float32
        ),
        "mp",
        scatter_dimension=0,
        tiled=True,
    )
    values = tokens.astype(jnp.float32)
    scale = lax.rsqrt(jnp.mean(values * values, axis=1, keepdims=True) + 1e-06)
    gain_grad = lax.psum(jnp.sum(normed_grad * values * scale, axis=0), "mp")
    inner = jnp.mean(norm_gain[None, :] * normed_grad * values, axis=1, keepdims=True)
    tokens_grad = scale * norm_gain[None, :] * normed_grad - values * scale * scale * scale * inner
    tokens_grad, gain_grad, bias_grad = (tokens_grad, gain_grad, bias_grad)
    tokens_grad, later = lax.optimization_barrier((tokens_grad, tokens))
    normed = normalize(later, norm_gain)
    project_normed = lax.all_gather(normed, "mp", axis=0, tiled=True)
    joined = (
        jnp.dot(project_normed, qkv_weight, preferred_element_type=jnp.float32) + qkv_bias[None, :]
    )
    place = positions(project_normed.shape[0], stride)
    qkv = rotate_heads(joined, first_col, place, 1.0).astype(jnp.bfloat16)
    return (qkv, tokens_grad, gain_grad, bias_grad)


def solution(mesh):
    in_specs = (P(("dp", "mp"), None), P(), P(None, "mp"), P("mp"), P("dp", "mp"))
    out_specs = (P("dp", "mp"), P(("dp", "mp"), None), P("dp"), P(("dp", "mp")))
    return jax.shard_map(shards, mesh=mesh, in_specs=in_specs, out_specs=out_specs, check_vma=False)
```

profile of v0, /device:TPU:0, one launch (start us, length us, event | category | flops | bytes accessed | tf_op | source)
XLA Modules:
  0.0 186.8 jit_solution(11591648086676076548)
XLA Ops:
  7.2 0.0 reduce-scatter.2.cloned.1.call-start
  7.3 0.1 broadcast_in_dim.15
  7.4 0.1 broadcast_in_dim.16
  7.5 1.3 copy.9
  8.8 0.2 multiply_sine_fusion
  9.0 0.2 multiply_subtract_fusion.1
  9.2 0.1 pad_maximum_fusion
  9.4 0.0 copy-start.1
  9.4 0.4 copy.10
  9.8 0.7 copy-done.1
  10.5 20.4 %fusion.11 = f32[128,8192]{1,0:T(8,128)} fusion(bf16[8192,2560]{1,0:T(8,128)(2,1)} %param.7, f32[128,2560]{1,0:T(8,128)S(1)} %copy.10, pred[2560]{0:T(1024)(128)(4,1)S(1)} %broadcast_in_dim.16, bf16[128,2560]{1,0:T(8,128)(2,1)S(1)} %copy-done.1), kind=kOutput, calls=%fused_computation.23 | convolution fusion | flops 5369364480 | bytes 48105984 | tf_op jit(solution)/shard_map/dot_general | solution.py:52
  30.9 0.0 copy-start
  30.9 0.0 copy-start.3
  30.9 0.0 reduce-scatter.2.cloned.1.call-update
  30.9 0.0 all-gather.2.cloned.1.call-start
  31.0 1.0 copy-done
  32.0 0.2 fusion.3
  32.2 78.4 %reduce-scatter.2.cloned.1.call-done = f32[32,8192]{1,0:T(8,128)} async-done(((f32[128,8192]{1,0:T(8,128)}), f32[32,8192]{1,0:T(8,128)}) %reduce-scatter.2.cloned.1.call-update) | async-done | bytes 1048592 | tf_op jit(solution)/shard_map/reduce_scatter | solution.py:51
  110.6 0.0 copy-done.3
  110.6 0.0 copy-start.2
  110.6 1.7 fusion.10
  112.3 0.0 copy-done.2
  112.3 1.3 fusion.7
  113.7 0.2 fusion
  113.9 1.0 fusion.2
  114.9 0.0 copy-start.4
  114.9 0.0 all-gather.2.cloned.1.call-update
  114.9 0.8 fusion.13
  115.7 19.8 %psum.7 = f32[8192]{0:T(1024)} all-reduce(f32[8192]{0:T(1024)S(1)} %get-tuple-element.8), channel_id=1, replica_groups=mesh['dp'=8,'mp'=4] {'mp'}, use_global_device_ids=true, to_apply=%region_5.6 | all-reduce | flops 8192 | bytes 65536 | tf_op jit(solution)/shard_map/psum | solution.py:61
  135.5 26.1 %all-gather.2.cloned.1.call-done = bf16[128,8192]{1,0:T(8,128)(2,1)} async-done(((bf16[32,8192]{1,0:T(8,128)(2,1)}), bf16[128,8192]{1,0:T(8,128)(2,1)}) %all-gather.2.cloned.1.call-update) | async-done | bytes 2097168 | tf_op jit(solution)/shard_map/all_gather | solution.py:67
  161.6 0.0 copy-done.4
  161.6 16.4 %convolution_add_fusion = f32[128,2560]{1,0:T(8,128)S(1)} fusion(bf16[128,8192]{1,0:T(8,128)(2,1)} %all-gather.2.cloned.1.call-done, bf16[8192,2560]{1,0:T(8,128)(2,1)} %param.7, f32[2560]{0:T(1024)S(1)} %copy-done.4), kind=kOutput, calls=%fused_computation | convolution fusion | flops 5369036800 | bytes 45361152 | tf_op jit(solution)/shard_map/dot_general | solution.py:69
  178.0 0.4 copy.11
  178.4 0.2 multiply_subtract_fusion
  178.6 0.1 pad_maximum_fusion.1
  178.7 0.2 copy.12
  179.0 1.0 select_convert_fusion
  (6 shorter events, 0.1 us)
Async XLA Ops:
  7.2 103.4 %reduce-scatter.2.cloned.1.call-start = ((), (), s32[]{:S(2)}) async-start(), calls=%async_computation.1 | async-start | bytes 5242880 | tf_op jit(solution)/shard_map/reduce_scatter | solution.py:51
  9.4 1.1 copy-start.1
  30.9 1.0 copy-start
  30.9 79.7 %copy-start.3 = (f32[8192]{0:T(1024)S(1)}, f32[8192]{0:T(1024)}, u32[]{:S(2)}) copy-start(f32[8192]{0:T(1024)} %param.6) | copy-start | bytes 98308
  30.9 130.7 %all-gather.2.cloned.1.call-start = ((), (), s32[]{:S(2)}) async-start(), calls=%async_computation.2 | async-start | bytes 2621440 | tf_op jit(solution)/shard_map/all_gather | solution.py:67
  110.6 1.7 copy-start.2
  114.9 46.7 %copy-start.4 = (f32[2560]{0:T(1024)S(1)}, f32[2560]{0:T(1024)}, u32[]{:S(2)}) copy-start(f32[2560]{0:T(1024)} %param.8) | copy-start | bytes 30724
Sparse Core Ops, SparseCore 0:
  31.1 79.5 reduce-scatter.1
  115.0 46.5 all-gather.1
where the time goes:
time: 187 us
  waiting for transfers between devices  105 us (56%)
  matrix products  36.9 us (20%)
  blocking collectives  19.8 us (11%)
  between operations  14.2 us (8%)
  other arithmetic  7.08 us (4%)
  local copies, waits for them, and re-layouts  4.19 us (2%)
    reduce_scatter x1, waiting for transfers between devices, shards(): lax.psum_scatter(lax.dot_general(joined_low, qkv_weight, (((1,), (1,)), (...  78.4 us
    all_gather x1, waiting for transfers between devices, shards(): project_normed = lax.all_gather(normed, 'mp', axis=0, tiled=True)  26.1 us
    dot_general x1, matrix products, shards(): lax.dot_general(joined_low, qkv_weight, (((1,), (1,)), ((), ())), preferr...  20.4 us
    psum x1, blocking collectives, shards(): gain_grad = lax.psum(jnp.sum(normed_grad * values * scale, axis=0), 'mp')  19.8 us
    dot_general x1, matrix products, shards(): jnp.dot(project_normed, qkv_weight, preferred_element_type=jnp.float32)  16.4 us
  transfers between devices with their start and end apart: 2, of which 2 were waited for; matrix products, arithmetic and copies ran while one was open for 1% of the time, Pallas kernels for 0%

commit v1 on v0

--- a/solution.py
+++ b/solution.py
@@ -58,7 +58,7 @@
     )
     values = tokens.astype(jnp.float32)
     scale = lax.rsqrt(jnp.mean(values * values, axis=1, keepdims=True) + 1e-06)
-    gain_grad = lax.psum(jnp.sum(normed_grad * values * scale, axis=0), "mp")
+    gain_grad = jnp.sum(lax.all_gather(jnp.sum(normed_grad * values * scale, axis=0), "mp"), axis=0)
     inner = jnp.mean(norm_gain[None, :] * normed_grad * values, axis=1, keepdims=True)
     tokens_grad = scale * norm_gain[None, :] * normed_grad - values * scale * scale * scale * inner
     tokens_grad, gain_grad, bias_grad = (tokens_grad, gain_grad, bias_grad)

time: 187 us -> 187 us (level)
  blocking collectives: 19.8 us -> 14.5 us
  waiting for transfers between devices: 105 us -> 109 us
    psum x1 -> x0, blocking collectives: 19.8 us -> none  [shards(): gain_grad = lax.psum(jnp.sum(normed_grad * values * scale, axis=0), 'mp')]
    all_gather x0 -> x1, blocking collectives: none -> 14.5 us  [shards(): lax.all_gather(jnp.sum(normed_grad * values * scale, axis=0), 'mp')]
    all_gather x1, waiting for transfers between devices: 26.1 us -> 30.7 us  [shards(): project_normed = lax.all_gather(normed, 'mp', axis=0, tiled=True)]
where the time goes in v1:
time: 187 us
  waiting for transfers between devices  109 us (58%)
  matrix products  36.9 us (20%)
  blocking collectives  14.5 us (8%)
  between operations  14.2 us (8%)
  other arithmetic  7.77 us (4%)
  local copies, waits for them, and re-layouts  4.24 us (2%)
    reduce_scatter x1, waiting for transfers between devices, shards(): lax.psum_scatter(lax.dot_general(joined_low, qkv_weight, (((1,), (1,)), (...  78.4 us
    all_gather x1, waiting for transfers between devices, shards(): project_normed = lax.all_gather(normed, 'mp', axis=0, tiled=True)  30.7 us
    dot_general x1, matrix products, shards(): lax.dot_general(joined_low, qkv_weight, (((1,), (1,)), ((), ())), preferr...  20.4 us
    dot_general x1, matrix products, shards(): jnp.dot(project_normed, qkv_weight, preferred_element_type=jnp.float32)  16.4 us
    all_gather x1, blocking collectives, shards(): lax.all_gather(jnp.sum(normed_grad * values * scale, axis=0), 'mp')  14.5 us
  transfers between devices with their start and end apart: 2, of which 2 were waited for; matrix products, arithmetic and copies ran while one was open for 1% of the time, Pallas kernels for 0%

profile of v1, /device:TPU:0, one launch (start us, length us, event | category | flops | bytes accessed | tf_op | source)
XLA Modules:
  0.0 186.8 jit_solution(6070158731925100734)
XLA Ops:
  7.2 0.0 reduce-scatter.2.cloned.1.call-start
  7.3 0.1 broadcast_in_dim.15
  7.4 0.1 broadcast_in_dim.16
  7.5 1.3 copy.17
  8.8 0.2 multiply_sine_fusion
  9.0 0.2 multiply_subtract_fusion.1
  9.2 0.1 pad_maximum_fusion
  9.4 0.0 copy-start.1
  9.4 0.4 copy.18
  9.8 0.7 copy-done.1
  10.5 20.4 %fusion.11 = f32[128,8192]{1,0:T(8,128)} fusion(bf16[8192,2560]{1,0:T(8,128)(2,1)} %param.7, f32[128,2560]{1,0:T(8,128)S(1)} %copy.18, pred[2560]{0:T(1024)(128)(4,1)S(1)} %broadcast_in_dim.16, bf16[128,2560]{1,0:T(8,128)(2,1)S(1)} %copy-done.1), kind=kOutput, calls=%fused_computation.23 | convolution fusion | flops 5369364480 | bytes 48105984 | tf_op jit(solution)/shard_map/dot_general | solution.py:52
  30.9 0.0 copy-start
  30.9 0.0 copy-start.3
  30.9 0.0 reduce-scatter.2.cloned.1.call-update
  30.9 0.0 all-gather.3.cloned.1.call-start
  31.0 1.0 copy-done
  32.0 0.2 fusion.3
  32.2 78.4 %reduce-scatter.2.cloned.1.call-done = f32[32,8192]{1,0:T(8,128)} async-done(((f32[128,8192]{1,0:T(8,128)}), f32[32,8192]{1,0:T(8,128)}) %reduce-scatter.2.cloned.1.call-update) | async-done | bytes 1048592 | tf_op jit(solution)/shard_map/reduce_scatter | solution.py:51
  110.6 0.0 copy-done.3
  110.6 0.0 copy-start.2
  110.6 1.7 fusion.10
  112.3 0.0 copy-done.2
  112.3 1.3 fusion.7
  113.7 0.2 fusion
  113.9 1.0 fusion.2
  114.9 0.0 all-gather.3.cloned.1.call-update
  114.9 0.0 copy-start.4
  114.9 0.8 fusion.13
  115.7 14.5 %all-gather = f32[32768]{0:T(1024)S(1)} all-gather(f32[8192]{0:T(1024)S(1)} %get-tuple-element.8), channel_id=2, replica_groups=mesh['dp'=8,'mp'=4] {'mp'}, dimensions={0}, use_global_device_ids=true | all-gather | bytes 163840 | tf_op jit(solution)/shard_map/all_gather | solution.py:61
  130.2 0.7 reduce_sum.58
  130.9 30.7 %all-gather.3.cloned.1.call-done = bf16[128,8192]{1,0:T(8,128)(2,1)} async-done(((bf16[32,8192]{1,0:T(8,128)(2,1)}), bf16[128,8192]{1,0:T(8,128)(2,1)}) %all-gather.3.cloned.1.call-update) | async-done | bytes 2097168 | tf_op jit(solution)/shard_map/all_gather | solution.py:67
  161.6 0.0 copy-done.4
  161.6 16.4 %convolution_add_fusion = f32[128,2560]{1,0:T(8,128)S(1)} fusion(bf16[128,8192]{1,0:T(8,128)(2,1)} %all-gather.3.cloned.1.call-done, bf16[8192,2560]{1,0:T(8,128)(2,1)} %param.7, f32[2560]{0:T(1024)S(1)} %copy-done.4), kind=kOutput, calls=%fused_computation | convolution fusion | flops 5369036800 | bytes 45361152 | tf_op jit(solution)/shard_map/dot_general | solution.py:69
  178.0 0.4 copy.19
  178.4 0.2 multiply_subtract_fusion
  178.6 0.1 pad_maximum_fusion.1
  178.7 0.2 copy.20
  179.0 1.0 select_convert_fusion
  (7 shorter events, 0.1 us)
Async XLA Ops:
  7.2 103.4 %reduce-scatter.2.cloned.1.call-start = ((), (), s32[]{:S(2)}) async-start(), calls=%async_computation.1 | async-start | bytes 5242880 | tf_op jit(solution)/shard_map/reduce_scatter | solution.py:51
  9.4 1.1 copy-start.1
  30.9 1.0 copy-start
  30.9 79.7 %copy-start.3 = (f32[8192]{0:T(1024)S(1)}, f32[8192]{0:T(1024)}, u32[]{:S(2)}) copy-start(f32[8192]{0:T(1024)} %param.6) | copy-start | bytes 98308
  30.9 130.7 %all-gather.3.cloned.1.call-start = ((), (), s32[]{:S(2)}) async-start(), calls=%async_computation.2 | async-start | bytes 2621440 | tf_op jit(solution)/shard_map/all_gather | solution.py:67
  110.6 1.7 copy-start.2
  114.9 46.7 %copy-start.4 = (f32[2560]{0:T(1024)S(1)}, f32[2560]{0:T(1024)}, u32[]{:S(2)}) copy-start(f32[2560]{0:T(1024)} %param.8) | copy-start | bytes 30724
Sparse Core Ops, SparseCore 0:
  31.1 79.5 reduce-scatter.1
  115.0 46.5 all-gather.2
